TPU v7x, 256 devices: a 2x2x32 block of a 4x8x32 slice. The times are simulated.
256 devices in a mesh: gp: 4 (over y, x), blk: 64 (over z, core).
Axes of the slice: x: 2, y: 2, z: 32, core: 2. Of those that a mesh axis runs over, the one named last changes fastest.
The devices are a block of a 4x8x32 slice.
Arguments:
- points: float32 [8, 65536], P(None, ('gp', 'blk')), parts along dimension 1, may hold values from -6 to 6
- vectors: float32 [8, 65536], P(None, ('gp', 'blk')), parts along dimension 1, may hold values from -6 to 6
- inv_length: float32 [32], P('gp'), parts along dimension 0, may hold values from 0.15 to 0.6
- noise: float32 [4], P('gp'), parts along dimension 0, may hold values from 0.1 to 1
Outputs:
- product: float32 [8, 65536], P(None, ('gp', 'blk')), parts along dimension 1
There are 4 independent parts, one for each index of `gp`. A program takes and returns all parts, laid end to end along the dimension named above; each array names one. Nothing has to cross between parts.
All inputs are finite; a program needn't handle non-finite values.
Results may differ from a plain program's by a relative error of at most 0.00017.
Values sent between devices are 32-bit elements; how exact they have to be, the bound alone decides.
A program may use at most 64 MiB of HBM per device.

v0:
```python
import jax
import jax.numpy as jnp
from jax import lax
from jax.sharding import PartitionSpec as P


def matern(left, right, inv_length):
    scaled_left = left * inv_length[:, None]
    scaled_right = right * inv_length[:, None]
    sq_left = jnp.sum(scaled_left * scaled_left, axis=0)
    sq_right = jnp.sum(scaled_right * scaled_right, axis=0)
    cross = jnp.dot(
        scaled_left.T,
        scaled_right,
        precision=lax.Precision.HIGHEST,
        preferred_element_type=jnp.float32,
    )
    dist2 = jnp.maximum(sq_left[:, None] + sq_right[None, :] - 2.0 * cross, 0.0)
    scaled_dist = jnp.sqrt(5.0 * dist2)
    return (1.0 + scaled_dist + scaled_dist * scaled_dist / 3.0) * jnp.exp(-scaled_dist)


def apply_tile(vec_other, tile):
    return jnp.dot(
        vec_other, tile, precision=lax.Precision.HIGHEST, preferred_element_type=jnp.float32
    )


def on_device(points, vectors, inv_length, noise):
    count = lax.axis_size("blk")
    total_points = points.shape[1] * count
    tile = matern(lax.all_gather(points, "blk", axis=1, tiled=True), points, inv_length)
    own_sum = apply_tile(lax.all_gather(vectors, "blk", axis=1, tiled=True), tile)
    return noise[0] * vectors + own_sum / jnp.sqrt(jnp.float32(total_points))


def solution(mesh):
    return jax.shard_map(
        on_device,
        mesh=mesh,
        in_specs=(P(None, ("gp", "blk")), P(None, ("gp", "blk")), P("gp"), P("gp")),
        out_specs=P(None, ("gp", "blk")),
        check_vma=False,
    )
```

profile of v0, /device:TPU:37, one launch (start us, length us, event | category | flops | bytes accessed | tf_op | source)
XLA Modules:
  0.0 170.3 jit_solution(1310754627161676833)
XLA Ops:
  0.0 0.0 copy-start
  0.0 78.1 %all_gather.6 = f32[8,16384]{1,0:T(8,128)S(1)} all-gather(f32[8,256]{1,0:T(8,128)} %param.4), channel_id=1, replica_groups=mesh['gp'=4,'blk'=64] {'blk'}, dimensions={1}, use_global_device_ids=true | all-gather | bytes 532480 | tf_op jit(solution)/shard_map/all_gather | solution.py:32
  78.1 0.9 multiply_reduce_fusion
  79.0 0.8 multiply_reduce_fusion.1
  79.8 23.7 %fusion.3 = f32[16384,256]{1,0:T(8,128)S(1)} fusion(f32[256]{0:T(256)S(1)} %multiply_reduce_fusion.1, f32[16384]{0:T(1024)S(1)} %multiply_reduce_fusion, f32[8,16384]{1,0:T(8,128)S(1)} %all_gather.6, f32[8]{0:T(128)} %param.6, f32[8,256]{1,0:T(8,128)} %param.4), kind=kOutput, calls=%fused_computation.4 | convolution fusion | flops 423757824 | bytes 17376288 | tf_op jit(solution)/shard_map/dot_general | solution.py:12
  103.5 0.0 copy-done
  103.5 54.1 %all_gather.7 = f32[8,16384]{1,0:T(8,128)S(1)} all-gather(f32[8,256]{1,0:T(8,128)S(1)} %copy-done), channel_id=1, replica_groups=mesh['gp'=4,'blk'=64] {'blk'}, dimensions={1}, use_global_device_ids=true | all-gather | bytes 532480 | tf_op jit(solution)/shard_map/all_gather | solution.py:33
  158.2 12.1 %fusion.20 = f32[8,256]{1,0:T(8,128)} fusion(f32[8,16384]{1,0:T(8,128)S(1)} %all_gather.7, f32[16384,256]{1,0:T(8,128)S(1)} %fusion.3, f32[8,256]{1,0:T(8,128)S(1)} %copy-done, f32[]{:T(128)} %bitcast.6), kind=kOutput, calls=%fused_computation.17 | convolution fusion | flops 427825152 | bytes 17317892 | tf_op jit(solution)/shard_map/dot_general | solution.py:24
Async XLA Ops:
  0.0 103.5 %copy-start = (f32[8,256]{1,0:T(8,128)S(1)}, f32[8,256]{1,0:T(8,128)}, u32[]{:S(2)}) copy-start(f32[8,256]{1,0:T(8,128)} %param.5) | copy-start | bytes 24580
where the time goes:
time: 171 us; the launch traced here: 170 us
  blocking collectives  132 us (77%)
  matrix products  35.8 us (21%)
    all_gather x1, blocking collectives, on_device(): lax.all_gather(points, 'blk', axis=1, tiled=True)  78.1 us
    all_gather x1, blocking collectives, on_device(): lax.all_gather(vectors, 'blk', axis=1, tiled=True)  54.1 us
    dot_general x1, matrix products, matern(): jnp.dot(scaled_left.T, scaled_right, precision=lax.Precision.HIGHEST, pre...  23.7 us
    dot_general x1, matrix products, apply_tile(): jnp.dot(vec_other, tile, precision=lax.Precision.HIGHEST, preferred_eleme...  12.1 us

commit v1 on v0

--- a/solution.py
+++ b/solution.py
@@ -2,6 +2,14 @@
 import jax.numpy as jnp
 from jax import lax
 from jax.sharding import PartitionSpec as P
+
+
+def gather_by_exchange(value, axis, dim):
+    size = lax.axis_size(axis)
+    repeats = [size if d == dim else 1 for d in range(value.ndim)]
+    return lax.all_to_all(
+        jnp.tile(value, repeats), axis, split_axis=dim, concat_axis=dim, tiled=True
+    )
 
 
 def matern(left, right, inv_length):
@@ -29,7 +37,7 @@
 def on_device(points, vectors, inv_length, noise):
     count = lax.axis_size("blk")
     total_points = points.shape[1] * count
-    tile = matern(lax.all_gather(points, "blk", axis=1, tiled=True), points, inv_length)
+    tile = matern(gather_by_exchange(points, "blk", 1), points, inv_length)
     own_sum = apply_tile(lax.all_gather(vectors, "blk", axis=1, tiled=True), tile)
     return noise[0] * vectors + own_sum / jnp.sqrt(jnp.float32(total_points))
 

time: 171 us -> 173 us (1.012)
  starting transfers between devices: 0 us -> 34.3 us
  blocking collectives: 132 us -> 97.8 us
    all_gather x1 -> x0, blocking collectives: 78.1 us -> none  [on_device(): lax.all_gather(points, 'blk', axis=1, tiled=True)]
    all_gather x1, blocking collectives: 54.1 us -> 97.8 us  [on_device(): lax.all_gather(vectors, 'blk', axis=1, tiled=True)]
    all_to_all x0 -> x1, starting transfers between devices: none -> 34.3 us  [gather_by_exchange(): lax.all_to_all(jnp.tile(value, repeats), axis, split_axis=dim, concat_axi...]
  transfers between devices with their start and end apart: 0 -> 1, of which waited for: 0 -> 0; matrix products, arithmetic and copies ran while one was open for 0% -> 0% of each run, Pallas kernels for 0% -> 0%
where the time goes in v1:
time: 173 us; the launch traced here: 172 us
  blocking collectives  97.8 us (57%)
  matrix products  36.1 us (21%)
  starting transfers between devices  34.3 us (20%)
    all_gather x1, blocking collectives, on_device(): lax.all_gather(vectors, 'blk', axis=1, tiled=True)  97.8 us
    all_to_all x1, starting transfers between devices, gather_by_exchange(): lax.all_to_all(jnp.tile(value, repeats), axis, split_axis=dim, concat_axi...  34.3 us
    dot_general x1, matrix products, matern(): jnp.dot(scaled_left.T, scaled_right, precision=lax.Precision.HIGHEST, pre...  24 us
    dot_general x1, matrix products, apply_tile(): jnp.dot(vec_other, tile, precision=lax.Precision.HIGHEST, preferred_eleme...  12.1 us
  transfers between devices with their start and end apart: 1, of which 0 were waited for; matrix products, arithmetic and copies ran while one was open for 0% of the time, Pallas kernels for 0%

profile of v1, /device:TPU:37, one launch (start us, length us, event | category | flops | bytes accessed | tf_op | source)
XLA Modules:
  0.0 172.2 jit_solution(3347644368773600278)
XLA Ops:
  0.0 0.0 copy-start
  0.0 1.5 tile.2
  1.5 34.3 %all-to-all-start = ((f32[8,64,256]{2,0,1:T(8,128)}), f32[8,64,256]{2,0,1:T(8,128)S(1)}, u32[]{:S(2)}, u32[]{:S(2)}) async-start(f32[8,64,256]{2,0,1:T(8,128)} %tile.2), calls=%async_computation | async-start | bytes 1048576 | tf_op jit(solution)/shard_map/all_to_all | solution.py:10
  36.5 0.8 multiply_reduce_fusion.1
  37.3 97.8 %all_gather.3 = f32[8,16384]{1,0:T(8,128)S(1)} all-gather(f32[8,256]{1,0:T(8,128)} %param.5), channel_id=1, replica_groups=mesh['gp'=4,'blk'=64] {'blk'}, dimensions={1}, use_global_device_ids=true | all-gather | bytes 532480 | tf_op jit(solution)/shard_map/all_gather | solution.py:41
  135.1 0.0 all-to-all-done
  135.1 0.9 multiply_reduce_fusion
  136.1 24.0 %fusion.3 = f32[16384,256]{1,0:T(8,128)S(1)} fusion(f32[256]{0:T(256)S(1)} %multiply_reduce_fusion.1, f32[16384]{0:T(1024)S(1)} %bitcast.12, f32[8,16384]{1,0:T(8,128)S(1)} %bitcast.10, f32[8]{0:T(128)} %param.6, f32[8,256]{1,0:T(8,128)} %param.4), kind=kOutput, calls=%fused_computation.4 | convolution fusion | flops 423757824 | bytes 17376288 | tf_op jit(solution)/shard_map/dot_general | solution.py:20
  160.1 0.0 copy-done
  160.1 12.1 %fusion.20 = f32[8,256]{1,0:T(8,128)} fusion(f32[8,16384]{1,0:T(8,128)S(1)} %all_gather.3, f32[16384,256]{1,0:T(8,128)S(1)} %fusion.3, f32[8,256]{1,0:T(8,128)S(1)} %copy-done, f32[]{:T(128)} %bitcast.9), kind=kOutput, calls=%fused_computation.17 | convolution fusion | flops 427825152 | bytes 17317892 | tf_op jit(solution)/shard_map/dot_general | solution.py:32
  (1 shorter events, 0.0 us)
Async XLA Ops:
  0.0 160.1 %copy-start = (f32[8,256]{1,0:T(8,128)S(1)}, f32[8,256]{1,0:T(8,128)}, u32[]{:S(2)}) copy-start(f32[8,256]{1,0:T(8,128)} %param.5) | copy-start | bytes 24580
  1.5 133.6 %all-to-all-start = ((f32[8,64,256]{2,0,1:T(8,128)}), f32[8,64,256]{2,0,1:T(8,128)S(1)}, u32[]{:S(2)}, u32[]{:S(2)}) async-start(f32[8,64,256]{2,0,1:T(8,128)} %tile.2), calls=%async_computation | async-start | bytes 1048576 | tf_op jit(solution)/shard_map/all_to_all | solution.py:10
